TPU v7x, 32 devices: a whole 2x2x4 slice. The times are simulated.
32 devices in a mesh: dp: 8 (over z, core), expert: 4 (over y, x).
Axes of the slice: x: 2, y: 2, z: 4, core: 2. Of those that a mesh axis runs over, the one named last changes fastest.
Arguments:
- mamba_in: bfloat16 [8, 256, 4096], P('dp'), may hold values from -6 to 6
- conv_state: bfloat16 [8, 3, 8192], P('dp', None, 'expert'), may hold values from -6 to 6
- in_weight: bfloat16 [4096, 8192], P('dp', 'expert'), may hold values from -0.09375 to 0.09375
- conv_kernel: float32 [4, 8192], P(None, 'expert'), may hold values from -3 to 3
- conv_bias: float32 [8192], P('expert'), may hold values from -1 to 1
- moe_in: bfloat16 [512, 4096], P('expert'), may hold values from -6 to 6
- router: bfloat16 [4096, 4], replicated, may hold values from -0.09375 to 0.09375
- expert_ids: int32 [512, 2], P('expert'), may hold values from 0 to 3, all different within a row; in each aligned block of 128 rows (0 to 127, 128 to 255, ...) at most 128 rows name the same one
- w_gate: bfloat16 [4, 4096, 12288], P('expert', None, 'dp'), may hold values from -0.09375 to 0.09375
- w_up: bfloat16 [4, 4096, 12288], P('expert', None, 'dp'), may hold values from -0.09375 to 0.09375
- w_down: bfloat16 [4, 12288, 4096], P('expert', 'dp'), may hold values from -0.078125 to 0.078125
Outputs:
- conv_out: bfloat16 [8, 256, 8192], P('dp', None, 'expert')
- moe_out: bfloat16 [512, 4096], P('expert', 'dp')
Inputs may be any that keep to these rules, and one draw needn't show every extreme that they name: `expert_ids`: each row names two different experts; among the 128 rows of one index of expert no expert is named more than 128 times, a bound that some block reaches.
All inputs are finite; a program needn't handle non-finite values.
Results may differ from a plain program's by a relative error of at most 0.0049.
Values may be sent and summed in bfloat16 or wider, within the bound.
No kernel may reach another device: no remote copies, remote signals or barrier semaphores. Data moves between devices by JAX's collectives and lax.ppermute only.
A program may use at most 192 MiB of HBM per device.

v0:
```python
import jax
import jax.numpy as jnp
from jax import lax
from jax.sharding import PartitionSpec as P


def expert_ffn(inputs, gate_mat, up_mat, down_mat):
    gate_val = jnp.dot(inputs, gate_mat, preferred_element_type=jnp.float32)
    up_val = jnp.dot(inputs, up_mat, preferred_element_type=jnp.float32)
    hidden = (jax.nn.silu(gate_val) * up_val).astype(jnp.bfloat16)
    return jnp.dot(hidden, down_mat, preferred_element_type=jnp.float32)


def body(
    mamba_in,
    conv_state,
    in_weight,
    conv_kernel,
    conv_bias,
    moe_in,
    router,
    expert_ids,
    w_gate,
    w_up,
    w_down,
):
    token_count = mamba_in.shape[1]
    width = mamba_in.shape[2]
    window = mamba_in.reshape(token_count, width)
    channels = in_weight.shape[1]
    taps = conv_kernel.shape[0]
    summed_proj = jnp.dot(
        window,
        lax.all_gather(in_weight, "dp", axis=0, tiled=True),
        preferred_element_type=jnp.float32,
    )
    projected = summed_proj.astype(jnp.bfloat16)
    extended = jnp.concatenate([conv_state[0], projected], axis=0)
    summed = jnp.zeros((token_count, channels), jnp.float32) + conv_bias[None, :]
    for offset in range(taps):
        summed = (
            summed
            + extended[offset : offset + token_count].astype(jnp.float32)
            * conv_kernel[offset][None, :]
        )
    conv_out = jax.nn.silu(summed).astype(jnp.bfloat16).reshape(1, token_count, channels)
    moe_rows = moe_in.shape[0]
    experts = lax.axis_size("expert") * w_gate.shape[0]
    capacity = min(moe_rows, 4 * moe_rows // experts)
    expert_range = jnp.arange(experts, dtype=jnp.int32)
    onehot_ids = (expert_ids.reshape(-1)[:, None] == expert_range[None, :]).astype(jnp.int32)
    earlier = jnp.cumsum(onehot_ids, axis=0) - onehot_ids
    slots = jnp.sum(earlier * onehot_ids, axis=1).reshape(moe_rows, 2)
    targets = expert_ids * capacity + slots
    slot_range = jnp.arange(experts * capacity, dtype=jnp.int32)
    first_hit = targets[:, 0][None, :] == slot_range[:, None]
    second_hit = targets[:, 1][None, :] == slot_range[:, None]
    dispatch_table = jnp.logical_or(first_hit, second_hit).astype(jnp.bfloat16)
    send_buffer = jnp.dot(dispatch_table, moe_in, preferred_element_type=jnp.float32).astype(
        jnp.bfloat16
    )
    send_buffer = send_buffer.reshape(experts, capacity, width)
    logits = jnp.dot(moe_in, router, preferred_element_type=jnp.float32)
    chosen_mask = (expert_ids[:, :, None] == expert_range[None, None, :]).astype(jnp.float32)
    chosen = jnp.sum(logits[:, None, :] * chosen_mask, axis=2)
    first_weight = jax.nn.sigmoid(chosen[:, 0] - chosen[:, 1])
    combine_table = first_weight[:, None] * first_hit.T.astype(jnp.float32) + (1.0 - first_weight)[
        :, None
    ] * second_hit.T.astype(jnp.float32)
    received = lax.all_to_all(send_buffer, "expert", split_axis=0, concat_axis=0, tiled=True)
    flat_rows = received.reshape(-1, width)
    result = expert_ffn(flat_rows, w_gate[0], w_up[0], w_down[0])
    partials = result.reshape(received.shape[0], received.shape[1], width)
    shares = lax.psum_scatter(partials, "dp", scatter_dimension=2, tiled=True)
    returned = lax.all_to_all(shares, "expert", split_axis=0, concat_axis=0, tiled=True)
    flat_back = returned.reshape(experts * capacity, returned.shape[2])
    mixed = jnp.dot(
        combine_table,
        flat_back,
        precision=lax.Precision.HIGHEST,
        preferred_element_type=jnp.float32,
    )
    return (conv_out, mixed.astype(jnp.bfloat16))


def solution(mesh):
    in_specs = (
        P("dp", None, None),
        P("dp", None, "expert"),
        P("dp", "expert"),
        P(None, "expert"),
        P("expert"),
        P("expert", None),
        P(),
        P("expert", None),
        P("expert", None, "dp"),
        P("expert", None, "dp"),
        P("expert", "dp", None),
    )
    out_specs = (P("dp", None, "expert"), P("expert", "dp"))
    return jax.shard_map(body, mesh=mesh, in_specs=in_specs, out_specs=out_specs, check_vma=False)
```

profile of v0, /device:TPU:0, one launch (start us, length us, event | category | flops | bytes accessed | tf_op | source)
XLA Modules:
  0.0 353.5 jit_solution(8871153900584539604)
XLA Ops:
  7.2 0.0 copy-start
  7.2 0.0 reduce-scatter.2.cloned.1.call-start
  7.2 0.9 copy.39
  8.2 0.1 eq.86
  8.3 0.1 eq.82
  8.4 1.2 reduce-window.6
  9.7 0.1 slice.56
  9.7 0.1 copy.41
  9.9 0.1 copy.42
  10.0 0.1 add_bitcast_fusion
  10.1 0.1 reshape.49
  10.2 0.1 copy.43
  10.3 0.7 multiply_add_fusion
  11.0 0.0 copy-start.6
  11.0 2.6 convolution_convert_fusion
  13.6 0.0 slice-start
  13.6 53.1 %all_to_all.10 = bf16[4,128,4096]{2,1,0:T(8,128)(2,1)S(1)} all-to-all(bf16[4,128,4096]{2,1,0:T(8,128)(2,1)S(1)} %bitcast.62), channel_id=1, replica_groups=mesh['dp'=8,'expert'=4] {'expert'}, dimensions={0} | all-to-all | bytes 8388608 | tf_op jit(solution)/shard_map/all_to_all | solution.py:70
  66.7 0.0 copy-done.6
  66.7 0.0 slice-start.1
  66.7 0.0 slice-start.2
  66.7 8.3 %fusion.4 = f32[512,1536]{1,0:T(8,128)} fusion(bf16[512,4096]{1,0:T(8,128)(2,1)S(1)} %bitcast.63, bf16[1,4096,1536]{2,1,0:T(8,128)(2,1)S(1)} %copy-done.6), kind=kOutput, calls=%fused_computation.4 | convolution fusion | flops 6442450944 | bytes 19922944 | tf_op jit(solution)/shard_map/dot_general | solution.py:8
  75.0 0.0 slice-done
  75.0 0.0 slice-done.1
  75.0 0.0 slice-done.2
  75.0 8.5 %fusion.9 = bf16[512,1536]{1,0:T(8,128)(2,1)S(1)} fusion(bf16[512,4096]{1,0:T(8,128)(2,1)S(1)} %bitcast.64, bf16[1,4096,1536]{2,1,0:T(8,128)(2,1)S(1)} %bitcast.74, f32[512,1536]{1,0:T(8,128)} %fusion.4), kind=kOutput, calls=%fused_computation.8 | convolution fusion | flops 6447169536 | bytes 21495808 | tf_op jit(solution)/shard_map/dot_general | solution.py:9
  83.5 11.8 %fusion = f32[4,128,4096]{2,1,0:T(8,128)} fusion(bf16[4,128,1536]{2,1,0:T(8,128)(2,1)S(1)} %bitcast.75, bf16[1,1536,4096]{2,1,0:T(8,128)(2,1)} %param.21), kind=kOutput, calls=%fused_computation | convolution fusion | flops 6442450944 | bytes 22544384 | tf_op jit(solution)/shard_map/dot_general | solution.py:11
  95.3 0.0 reduce-scatter.2.cloned.1.call-update
  95.4 0.0 copy-start.1
  95.4 0.0 all-gather.2.cloned.1.call-start
  95.4 0.7 all-gather.2.cloned.1.call-update
  96.1 0.0 copy-start.4
  96.1 0.0 copy-start.2
  96.2 88.7 %reduce-scatter.2.cloned.1.call-done = f32[4,128,512]{2,1,0:T(8,128)} async-done(((f32[4,128,4096]{2,1,0:T(8,128)}), f32[4,128,512]{2,1,0:T(8,128)}) %reduce-scatter.2.cloned.1.call-update) | async-done | bytes 1048592 | tf_op jit(solution)/shard_map/reduce_scatter | solution.py:74
  184.8 3.7 %all-to-all-start.1 = ((f32[4,128,512]{2,1,0:T(8,128)}), f32[4,128,512]{2,1,0:T(8,128)S(1)}, u32[]{:S(2)}, u32[]{:S(2)}) async-start(f32[4,128,512]{2,1,0:T(8,128)} %reduce-scatter.2.cloned.1.call-done), calls=%async_computation.2 | async-start | bytes 2097152 | tf_op jit(solution)/shard_map/all_to_all | solution.py:75
  188.5 0.0 copy-done.1
  188.6 1.6 fusion.33
  190.2 0.0 copy-done.4
  190.2 0.0 copy-done.2
  190.2 9.9 %all-to-all-done.1 = f32[4,128,512]{2,1,0:T(8,128)S(1)} async-done(((f32[4,128,512]{2,1,0:T(8,128)}), f32[4,128,512]{2,1,0:T(8,128)S(1)}, u32[]{:S(2)}, u32[]{:S(2)}) %all-to-all-start.1) | async-done | bytes 1048608 | tf_op jit(solution)/shard_map/all_to_all | solution.py:75
  200.1 1.4 convolution_convert_fusion.2
  201.5 0.0 copy-start.3
  201.5 0.0 copy-start.5
  201.5 134.5 %all-gather.2.cloned.1.call-done = bf16[4096,2048]{1,0:T(8,128)(2,1)} async-done(((bf16[512,2048]{1,0:T(8,128)(2,1)}), bf16[4096,2048]{1,0:T(8,128)(2,1)}) %all-gather.2.cloned.1.call-update) | async-done | bytes 16777232 | tf_op jit(solution)/shard_map/all_gather | solution.py:34
  336.0 0.0 copy-done
  336.0 8.3 %convolution_convert_fusion.1 = bf16[256,2048]{1,0:T(8,128)(2,1)S(1)} fusion(bf16[4096,2048]{1,0:T(8,128)(2,1)} %all-gather.2.cloned.1.call-done, bf16[1,256,4096]{2,1,0:T(8,128)(2,1)S(1)} %copy-done), kind=kOutput, calls=%fused_computation.9 | convolution fusion | flops 4295491584 | bytes 19922944 | tf_op jit(solution)/shard_map/dot_general | solution.py:32
  344.3 0.0 copy-done.3
  344.3 0.0 copy-done.5
  344.3 2.3 fusion.15
  (9 shorter events, 0.1 us)
Async XLA Ops:
  7.2 328.8 %copy-start = (bf16[1,256,4096]{2,1,0:T(8,128)(2,1)S(1)}, bf16[1,256,4096]{2,1,0:T(8,128)(2,1)}, u32[]{:S(2)}) copy-start(bf16[1,256,4096]{2,1,0:T(8,128)(2,1)} %param.11) | copy-start | bytes 6291460
  7.2 177.7 %reduce-scatter.2.cloned.1.call-start = ((), (), s32[]{:S(2)}) async-start(), calls=%async_computation.4 | async-start | bytes 9437184 | tf_op jit(solution)/shard_map/reduce_scatter | solution.py:74
  11.0 55.7 %copy-start.6 = (bf16[1,4096,1536]{2,1,0:T(8,128)(2,1)S(1)}, bf16[1,4096,1536]{2,1,0:T(8,128)(2,1)}, u32[]{:S(2)}) copy-start(bf16[1,4096,1536]{2,1,0:T(8,128)(2,1)} %param.19) | copy-start | bytes 37748740
  13.6 61.4 %slice-start = ((s8[12582912]{0:T(1024)(128)(4,1)}), s8[4194304]{0:T(1024)(128)(4,1)S(1)}, s32[]{:S(2)}) async-start(s8[12582912]{0:T(1024)(128)(4,1)} %bitcast.73), calls=%async_computation.5 | async-start | bytes 8388608
  66.7 8.3 %slice-start.1 = ((s8[12582912]{0:T(1024)(128)(4,1)}), s8[4194304]{0:T(1024)(128)(4,1)S(1)}, s32[]{:S(2)}) async-start(s8[12582912]{0:T(1024)(128)(4,1)} %bitcast.73), calls=%async_computation.6 | async-start | bytes 8388608
  66.7 8.3 %slice-start.2 = ((s8[12582912]{0:T(1024)(128)(4,1)}), s8[4194304]{0:T(1024)(128)(4,1)S(1)}, s32[]{:S(2)}) async-start(s8[12582912]{0:T(1024)(128)(4,1)} %bitcast.73), calls=%async_computation.7 | async-start | bytes 8388608
  95.4 93.2 %copy-start.1 = (bf16[4096,4]{0,1:T(4,128)(2,1)S(1)}, bf16[4096,4]{0,1:T(4,128)(2,1)}, u32[]{:S(2)}) copy-start(bf16[4096,4]{0,1:T(4,128)(2,1)} %param.17) | copy-start | bytes 98308
  95.4 240.6 %all-gather.2.cloned.1.call-start = ((), (), s32[]{:S(2)}) async-start(), calls=%async_computation.3 | async-start | bytes 18874368 | tf_op jit(solution)/shard_map/all_gather | solution.py:34
  96.1 94.0 %copy-start.4 = (s32[128,2]{0,1:T(2,128)S(1)}, s32[128,2]{0,1:T(2,128)}, u32[]{:S(2)}) copy-start(s32[128,2]{0,1:T(2,128)} %param.18) | copy-start | bytes 3076
  96.1 94.1 %copy-start.2 = (f32[4,2048]{1,0:T(4,128)S(1)}, f32[4,2048]{1,0:T(4,128)}, u32[]{:S(2)}) copy-start(f32[4,2048]{1,0:T(4,128)} %param.14) | copy-start | bytes 98308
  184.8 15.3 %all-to-all-start.1 = ((f32[4,128,512]{2,1,0:T(8,128)}), f32[4,128,512]{2,1,0:T(8,128)S(1)}, u32[]{:S(2)}, u32[]{:S(2)}) async-start(f32[4,128,512]{2,1,0:T(8,128)} %reduce-scatter.2.cloned.1.call-done), calls=%async_computation.2 | async-start | bytes 2097152 | tf_op jit(solution)/shard_map/all_to_all | solution.py:75
  201.5 142.7 %copy-start.3 = (bf16[1,3,2048]{2,1,0:T(4,128)(2,1)S(1)}, bf16[1,3,2048]{2,1,0:T(4,128)(2,1)}, u32[]{:S(2)}) copy-start(bf16[1,3,2048]{2,1,0:T(4,128)(2,1)} %param.12) | copy-start | bytes 36868
  201.5 142.7 %copy-start.5 = (f32[2048]{0:T(1024)S(1)}, f32[2048]{0:T(1024)}, u32[]{:S(2)}) copy-start(f32[2048]{0:T(1024)} %param.15) | copy-start | bytes 24580
Sparse Core Ops, SparseCore 0:
  95.5 89.3 reduce-scatter.1
  186.4 149.5 all-gather.1
where the time goes:
time: 354 us; the launch traced here: 353 us
  waiting for transfers between devices  234 us (66%)
  blocking collectives  53.1 us (15%)
  matrix products  42.5 us (12%)
  between operations  14.2 us (4%)
  other arithmetic  4.44 us (1%)
  starting transfers between devices  3.77 us (1%)
    all_gather x1, waiting for transfers between devices, body(): lax.all_gather(in_weight, 'dp', axis=0, tiled=True)  134 us
    reduce_scatter x1, waiting for transfers between devices, body(): shares = lax.psum_scatter(partials, 'dp', scatter_dimension=2, tiled=True)  88.7 us
    all_to_all x1, blocking collectives, body(): lax.all_to_all(send_buffer, 'expert', split_axis=0, concat_axis=0, tiled=...  53.1 us
    dot_general x1, matrix products, expert_ffn(): return jnp.dot(hidden, down_mat, preferred_element_type=jnp.float32)  11.8 us
    all_to_all x1, waiting for transfers between devices, body(): lax.all_to_all(shares, 'expert', split_axis=0, concat_axis=0, tiled=True)  9.86 us
    dot_general x1, matrix products, expert_ffn(): up_val = jnp.dot(inputs, up_mat, preferred_element_type=jnp.float32)  8.53 us
    dot_general x1, matrix products, expert_ffn(): gate_val = jnp.dot(inputs, gate_mat, preferred_element_type=jnp.float32)  8.28 us
    dot_general x1, matrix products, body(): jnp.dot(window, lax.all_gather(in_weight, 'dp', axis=0, tiled=True), pref...  8.25 us
  transfers between devices with their start and end apart: 3, of which 3 were waited for; matrix products, arithmetic and copies ran while one was open for 1% of the time, Pallas kernels for 0%

commit v1 on v0

--- a/solution.py
+++ b/solution.py
@@ -2,6 +2,29 @@
 import jax.numpy as jnp
 from jax import lax
 from jax.sharding import PartitionSpec as P
+
+
+def split_up(x, dim, size):
+    shape = x.shape
+    blocks = x.reshape(*shape[:dim], size, shape[dim] // size, *shape[dim + 1 :])
+    return jnp.moveaxis(blocks, dim, 0)
+
+
+def joined_along(parts, dim):
+    parts = jnp.moveaxis(parts, 0, dim)
+    shape = parts.shape
+    return parts.reshape(*shape[:dim], shape[dim] * shape[dim + 1], *shape[dim + 2 :])
+
+
+def pairwise_exchange(shard, axis, split_dim, concat_dim):
+    size, mine = (lax.axis_size(axis), lax.axis_index(axis))
+    blocks = split_up(shard, split_dim, size)
+    outs = [blocks[mine]]
+    for step in range(1, size):
+        sent = blocks[mine ^ step]
+        outs.append(lax.ppermute(sent, axis, [(i, i ^ step) for i in range(size)]))
+    blocks = jnp.stack(outs)[mine ^ jnp.arange(size)]
+    return joined_along(blocks, concat_dim)
 
 
 def expert_ffn(inputs, gate_mat, up_mat, down_mat):
@@ -72,7 +95,7 @@
     result = expert_ffn(flat_rows, w_gate[0], w_up[0], w_down[0])
     partials = result.reshape(received.shape[0], received.shape[1], width)
     shares = lax.psum_scatter(partials, "dp", scatter_dimension=2, tiled=True)
-    returned = lax.all_to_all(shares, "expert", split_axis=0, concat_axis=0, tiled=True)
+    returned = pairwise_exchange(shares, "expert", 0, 0)
     flat_back = returned.reshape(experts * capacity, returned.shape[2])
     mixed = jnp.dot(
         combine_table,

time: 354 us -> 353 us (level)
  waiting for transfers between devices: 234 us -> 230 us
    all_to_all x1 -> x0, waiting for transfers between devices: 9.86 us -> none  [body(): lax.all_to_all(shares, 'expert', split_axis=0, concat_axis=0, tiled=True)]
    ppermute x0 -> x3, waiting for transfers between devices: none -> 8.97 us  [pairwise_exchange(): outs.append(lax.ppermute(sent, axis, [(i, i ^ step) for i in range(size)]))]
    all_to_all x1 -> x0, starting transfers between devices: 3.7 us -> none  [body(): lax.all_to_all(shares, 'expert', split_axis=0, concat_axis=0, tiled=True)]
    ppermute x0 -> x3, starting transfers between devices: none -> 3.55 us  [pairwise_exchange(): outs.append(lax.ppermute(sent, axis, [(i, i ^ step) for i in range(size)]))]
  transfers between devices with their start and end apart: 3 -> 5, of which waited for: 3 -> 4; matrix products, arithmetic and copies ran while one was open for 1% -> 2% of each run, Pallas kernels for 0% -> 0%
where the time goes in v1:
time: 353 us
  waiting for transfers between devices  230 us (65%)
  blocking collectives  53.1 us (15%)
  matrix products  40.4 us (11%)
  between operations  14.2 us (4%)
  other arithmetic  5.49 us (2%)
  local copies, waits for them, and re-layouts  5.25 us (1%)
  starting transfers between devices  3.81 us (1%)
    all_gather x1, waiting for transfers between devices, body(): lax.all_gather(in_weight, 'dp', axis=0, tiled=True)  133 us
    reduce_scatter x1, waiting for transfers between devices, body(): shares = lax.psum_scatter(partials, 'dp', scatter_dimension=2, tiled=True)  87.8 us
    all_to_all x1, blocking collectives, body(): lax.all_to_all(send_buffer, 'expert', split_axis=0, concat_axis=0, tiled=...  53.1 us
    dot_general x1, matrix products, expert_ffn(): up_val = jnp.dot(inputs, up_mat, preferred_element_type=jnp.float32)  10.4 us
    ppermute x3, waiting for transfers between devices, pairwise_exchange(): outs.append(lax.ppermute(sent, axis, [(i, i ^ step) for i in range(size)]))  8.97 us
    dot_general x1, matrix products, expert_ffn(): return jnp.dot(hidden, down_mat, preferred_element_type=jnp.float32)  8.92 us
    dot_general x1, matrix products, expert_ffn(): gate_val = jnp.dot(inputs, gate_mat, preferred_element_type=jnp.float32)  8.32 us
    dot_general x1, matrix products, body(): jnp.dot(window, lax.all_gather(in_weight, 'dp', axis=0, tiled=True), pref...  8.25 us
  transfers between devices with their start and end apart: 5, of which 4 were waited for; matrix products, arithmetic and copies ran while one was open for 2% of the time, Pallas kernels for 0%

profile of v1, /device:TPU:0, one launch (start us, length us, event | category | flops | bytes accessed | tf_op | source)
XLA Modules:
  0.0 352.5 jit_solution(6554081577197939911)
XLA Ops:
  7.2 0.0 copy-start
  7.2 0.0 reduce-scatter.2.cloned.1.call-start
  7.2 0.9 copy.39
  8.2 0.1 eq.86
  8.3 0.1 eq.82
  8.4 1.2 reduce-window.6
  9.7 0.1 slice.58
  9.7 0.1 copy.41
  9.9 0.1 copy.42
  10.0 0.1 add_bitcast_fusion
  10.1 0.1 reshape.70
  10.2 0.1 copy.43
  10.3 0.7 multiply_add_fusion
  11.0 2.6 convolution_convert_fusion
  13.6 53.1 %all_to_all.5 = bf16[4,128,4096]{2,1,0:T(8,128)(2,1)S(1)} all-to-all(bf16[4,128,4096]{2,1,0:T(8,128)(2,1)S(1)} %bitcast.71), channel_id=1, replica_groups=mesh['dp'=8,'expert'=4] {'expert'}, dimensions={0} | all-to-all | bytes 8388608 | tf_op jit(solution)/shard_map/all_to_all | solution.py:93
  66.7 0.0 copy-done.7
  66.7 8.3 %fusion.4 = f32[512,1536]{1,0:T(8,128)} fusion(bf16[512,4096]{1,0:T(8,128)(2,1)S(1)} %bitcast.73, bf16[1,4096,1536]{2,1,0:T(8,128)(2,1)S(1)} %copy-done.7), kind=kOutput, calls=%fused_computation.5 | convolution fusion | flops 6442450944 | bytes 19922944 | tf_op jit(solution)/shard_map/dot_general | solution.py:31
  75.0 10.4 %fusion.9 = bf16[512,1536]{1,0:T(8,128)(2,1)S(1)} fusion(bf16[512,4096]{1,0:T(8,128)(2,1)S(1)} %bitcast.74, bf16[1,4096,1536]{2,1,0:T(8,128)(2,1)} %param.20, f32[512,1536]{1,0:T(8,128)} %fusion.4), kind=kOutput, calls=%fused_computation.9 | convolution fusion | flops 6447169536 | bytes 21495808 | tf_op jit(solution)/shard_map/dot_general | solution.py:32
  85.5 0.0 slice-done
  85.5 0.0 slice-done.1
  85.5 0.0 slice-done.2
  85.5 8.9 %fusion = f32[4,128,4096]{2,1,0:T(8,128)} fusion(bf16[4,128,1536]{2,1,0:T(8,128)(2,1)S(1)} %bitcast.87, bf16[1,1536,4096]{2,1,0:T(8,128)(2,1)S(1)} %bitcast.86), kind=kOutput, calls=%fused_computation.1 | convolution fusion | flops 6442450944 | bytes 22544384 | tf_op jit(solution)/shard_map/dot_general | solution.py:34
  94.5 0.0 reduce-scatter.2.cloned.1.call-update
  94.5 0.0 copy-start.1
  94.5 0.0 copy-start.2
  94.5 0.0 copy-start.5
  94.5 0.0 copy-start.3
  94.5 0.2 all-gather.2.cloned.1.call-start
  94.8 0.5 all-gather.2.cloned.1.call-update
  95.3 0.4 copy-done.1
  95.7 0.0 copy-done.2
  95.7 0.4 fusion.34
  96.2 87.8 %reduce-scatter.2.cloned.1.call-done = f32[4,128,512]{2,1,0:T(8,128)} async-done(((f32[4,128,4096]{2,1,0:T(8,128)}), f32[4,128,512]{2,1,0:T(8,128)}) %reduce-scatter.2.cloned.1.call-update) | async-done | bytes 1048592 | tf_op jit(solution)/shard_map/reduce_scatter | solution.py:97
  184.0 1.3 dynamic-slice_bitcast_fusion
  185.2 2.4 collective-permute-start.2
  187.7 0.6 collective-permute-start.1
  188.2 0.5 collective-permute-start
  188.8 6.2 %collective-permute-done.2 = f32[1,128,512]{2,1,0:T(8,128)S(1)} collective-permute-done((f32[1,128,512]{2,1,0:T(8,128)S(1)}, f32[1,128,512]{2,1,0:T(8,128)S(1)}, u32[]{:S(2)}, u32[]{:S(2)}) %collective-permute-start.2) | collective-permute-done | bytes 262176 | tf_op jit(solution)/shard_map/ppermute | solution.py:25
  195.0 2.7 collective-permute-done.1
  197.7 0.0 collective-permute-done
  197.8 1.0 maximum_bitcast_fusion
  198.8 1.8 gather_fusion
  200.6 1.4 convolution_convert_fusion.2
  202.1 133.0 %all-gather.2.cloned.1.call-done = bf16[4096,2048]{1,0:T(8,128)(2,1)} async-done(((bf16[512,2048]{1,0:T(8,128)(2,1)}), bf16[4096,2048]{1,0:T(8,128)(2,1)}) %all-gather.2.cloned.1.call-update) | async-done | bytes 16777232 | tf_op jit(solution)/shard_map/all_gather | solution.py:57
  335.1 8.3 %convolution_convert_fusion.1 = bf16[256,2048]{1,0:T(8,128)(2,1)S(1)} fusion(bf16[4096,2048]{1,0:T(8,128)(2,1)} %all-gather.2.cloned.1.call-done, bf16[1,256,4096]{2,1,0:T(8,128)(2,1)S(1)} %copy-done), kind=kOutput, calls=%fused_computation.10 | convolution fusion | flops 4295491584 | bytes 19922944 | tf_op jit(solution)/shard_map/dot_general | solution.py:55
  343.3 0.0 copy-done.4
  343.3 0.0 copy-done.6
  343.4 2.3 fusion.15
  (20 shorter events, 0.2 us)
Async XLA Ops:
  7.2 327.9 %copy-start = (bf16[1,256,4096]{2,1,0:T(8,128)(2,1)S(1)}, bf16[1,256,4096]{2,1,0:T(8,128)(2,1)}, u32[]{:S(2)}) copy-start(bf16[1,256,4096]{2,1,0:T(8,128)(2,1)} %param.11) | copy-start | bytes 6291460
  7.2 176.8 %reduce-scatter.2.cloned.1.call-start = ((), (), s32[]{:S(2)}) async-start(), calls=%async_computation.3 | async-start | bytes 9437184 | tf_op jit(solution)/shard_map/reduce_scatter | solution.py:97
  11.0 55.7 %copy-start.7 = (bf16[1,4096,1536]{2,1,0:T(8,128)(2,1)S(1)}, bf16[1,4096,1536]{2,1,0:T(8,128)(2,1)}, u32[]{:S(2)}) copy-start(bf16[1,4096,1536]{2,1,0:T(8,128)(2,1)} %param.19) | copy-start | bytes 37748740
  66.7 18.8 %slice-start = ((s8[12582912]{0:T(1024)(128)(4,1)}), s8[4194304]{0:T(1024)(128)(4,1)S(1)}, s32[]{:S(2)}) async-start(s8[12582912]{0:T(1024)(128)(4,1)} %bitcast.85), calls=%async_computation.4 | async-start | bytes 8388608
  66.7 18.8 %slice-start.1 = ((s8[12582912]{0:T(1024)(128)(4,1)}), s8[4194304]{0:T(1024)(128)(4,1)S(1)}, s32[]{:S(2)}) async-start(s8[12582912]{0:T(1024)(128)(4,1)} %bitcast.85), calls=%async_computation.5 | async-start | bytes 8388608
  75.0 10.5 %slice-start.2 = ((s8[12582912]{0:T(1024)(128)(4,1)}), s8[4194304]{0:T(1024)(128)(4,1)S(1)}, s32[]{:S(2)}) async-start(s8[12582912]{0:T(1024)(128)(4,1)} %bitcast.85), calls=%async_computation.6 | async-start | bytes 8388608
  94.5 1.2 copy-start.1
  94.5 1.2 copy-start.2
  94.5 1.6 copy-start.5
  94.5 1.6 copy-start.3
  94.5 240.5 %all-gather.2.cloned.1.call-start = ((), (), s32[]{:S(2)}) async-start(), calls=%async_computation.2 | async-start | bytes 18874368 | tf_op jit(solution)/shard_map/all_gather | solution.py:57
  185.2 9.8 %collective-permute-start.2 = (f32[1,128,512]{2,1,0:T(8,128)S(1)}, f32[1,128,512]{2,1,0:T(8,128)S(1)}, u32[]{:S(2)}, u32[]{:S(2)}) collective-permute-start(f32[1,128,512]{2,1,0:T(8,128)S(1)} %get-tuple-element.5), channel_id=1, source_target_pairs={{0,3},{1,2},{2,1},{3,0},{4,7},{5,6},{6,5},{7,4},{8,11},{9,10},{10,... | collective-permute-start | bytes 786440 | tf_op jit(solution)/shard_map/ppermute | solution.py:25
  187.7 10.1 %collective-permute-start.1 = (f32[1,128,512]{2,1,0:T(8,128)S(1)}, f32[1,128,512]{2,1,0:T(8,128)S(1)}, u32[]{:S(2)}, u32[]{:S(2)}) collective-permute-start(f32[1,128,512]{2,1,0:T(8,128)S(1)} %get-tuple-element.6), channel_id=1, source_target_pairs={{0,2},{1,3},{2,0},{3,1},{4,6},{5,7},{6,4},{7,5},{8,10},{9,11},{10,... | collective-permute-start | bytes 786440 | tf_op jit(solution)/shard_map/ppermute | solution.py:25
  188.2 9.5 %collective-permute-start = (f32[1,128,512]{2,1,0:T(8,128)S(1)}, f32[1,128,512]{2,1,0:T(8,128)S(1)}, u32[]{:S(2)}, u32[]{:S(2)}) collective-permute-start(f32[1,128,512]{2,1,0:T(8,128)S(1)} %get-tuple-element.7), channel_id=1, source_target_pairs={{0,1},{1,0},{2,3},{3,2},{4,5},{5,4},{6,7},{7,6},{8,9},{9,8},{10,11... | collective-permute-start | bytes 786440 | tf_op jit(solution)/shard_map/ppermute | solution.py:25
  202.1 141.3 %copy-start.4 = (bf16[1,3,2048]{2,1,0:T(4,128)(2,1)S(1)}, bf16[1,3,2048]{2,1,0:T(4,128)(2,1)}, u32[]{:S(2)}) copy-start(bf16[1,3,2048]{2,1,0:T(4,128)(2,1)} %param.12) | copy-start | bytes 36868
  202.1 141.3 %copy-start.6 = (f32[2048]{0:T(1024)S(1)}, f32[2048]{0:T(1024)}, u32[]{:S(2)}) copy-start(f32[2048]{0:T(1024)} %param.15) | copy-start | bytes 24580
Sparse Core Ops, SparseCore 0:
  94.6 89.3 reduce-scatter.1
  185.6 149.4 all-gather.1
